TPU v7x, 32 devices: a whole 2x2x4 slice. The times are simulated.
32 devices in a mesh: tm: 16 (over z, y, x), chan: 2 (over core).
Axes of the slice: x: 2, y: 2, z: 4, core: 2. Of those that a mesh axis runs over, the one named last changes fastest.
Arguments:
- spectrum: float32 [32, 131072], P('tm', 'chan'), may hold values from -6 to 6
- offsets: int32 [64], replicated, may hold values from 0 to 16, as said below
Outputs:
- peak: float32 [131072], P('chan')
Inputs may be any that keep to these rules, and one draw needn't show every extreme that they name: `offsets`: entries 0 and 1 are 0; entry 2L + d (drift d of the section that joins blocks of L) lies in 0 to L, and is exactly L for d = 2L - 1.
All inputs are finite; a program needn't handle non-finite values.
Results may differ from a plain program's by a relative error of at most 0.00002.
Values sent between devices are 32-bit elements; how exact they have to be, the bound alone decides.
A program may use at most 64 MiB of HBM per device.

v0:
```python
import functools

import jax
import jax.numpy as jnp
from jax import lax
from jax.experimental import pallas as pl
from jax.experimental.pallas import tpu as pltpu
from jax.sharding import PartitionSpec as P

LANES = 128
MESH = pl.DeviceIdType.MESH


def round_up(value, to):
    return (value + to - 1) // to * to


def flip(place, bits):
    out, bit = place, 1
    while bit <= bits:
        if bits & bit:
            out = out + bit * (1 - 2 * lax.rem(lax.div(place, bit), 2))
        bit *= 2
    return out


def kernel(count, chans, rows, tiles, halo, offs_ref, x_ref, out_ref, recv, *rest):
    levels = rest[:-5]
    send_sem, recv_sem, edge_sem, send_sem2, recv_sem2 = rest[-5:]
    me = lax.axis_index("tm")
    col = lax.axis_index("chan")
    total = count * rows
    body = tiles
    full = tiles + halo
    at_end = me == count - 1
    no_next = me * chans + col == count * chans - 1

    barrier = pltpu.get_barrier_semaphore()
    for j in range(1, count):
        pl.semaphore_signal(barrier, inc=1, device_id=(flip(me, j), col), device_id_type=MESH)
    if chans > 1:
        @pl.when(jnp.logical_and(at_end, col < chans - 1))
        def _():
            for t in range(count):
                pl.semaphore_signal(barrier, inc=1, device_id=(t, jnp.minimum(col + 1, chans - 1)), device_id_type=MESH)
    pl.semaphore_wait(barrier, count - 1 + jnp.where(col > 0, 1, 0))

    def to_peer(j, size):
        k = flip(me, j)
        return pltpu.make_async_remote_copy(
            src_ref=x_ref.at[pl.ds(k * body, size)],
            dst_ref=recv.at[me, pl.ds(0, size)],
            send_sem=send_sem.at[j],
            recv_sem=recv_sem.at[me],
            device_id=(k, col),
            device_id_type=MESH,
        )

    def both(j, act):
        @pl.when(flip(me, j) == count - 1)
        def _():
            act(to_peer(j, body))

        @pl.when(flip(me, j) != count - 1)
        def _():
            act(to_peer(j, full))

    def edge():
        return pltpu.make_async_remote_copy(
            src_ref=x_ref.at[pl.ds(0, halo)],
            dst_ref=recv.at[me, pl.ds(body, halo)],
            send_sem=edge_sem.at[0],
            recv_sem=recv_sem.at[me],
            device_id=(count - 1, jnp.maximum(col - 1, 0)),
            device_id_type=MESH,
        )

    def own(size):
        return pltpu.make_async_copy(
            x_ref.at[pl.ds(me * body, size)], recv.at[me, pl.ds(0, size)], recv_sem.at[me]
        )

    if chans > 1:
        @pl.when(col > 0)
        def _():
            edge().start()

    for j in reversed(range(1, count)):
        both(j, lambda copy: copy.start())

    @pl.when(at_end)
    def _():
        own(body).start()

    @pl.when(me != count - 1)
    def _():
        own(full).start()

    @pl.when(no_next)
    def _():
        for t in range(count):
            recv[t, pl.ds(body, halo)] = jnp.zeros((halo, rows, LANES), jnp.float32)

    def arrived(t):
        def wait(size):
            part = recv.at[t, pl.ds(0, size)]
            pltpu.make_async_copy(part, part, recv_sem.at[t]).wait()

        @pl.when(no_next)
        def _():
            wait(body)

        @pl.when(me * chans + col != count * chans - 1)
        def _():
            wait(full)

    def node(length, block, slot=0, inner=0):
        at = length.bit_length() - 1
        wide = tiles + (total - 2 * length + LANES - 1) // LANES
        lane = lax.broadcasted_iota(jnp.int32, (wide, LANES), 1)

        def load(which, d, start):
            if length == 1:
                return recv[slot, pl.ds(start, wide), 2 * inner + which]
            return levels[at - 1][2 * block + which, d, pl.ds(start, wide)]

        peak = None
        for half in range(length):
            low = load(0, half, 0)
            here = load(1, half, 0)
            ahead = load(1, half, 1)
            for d in (2 * half, 2 * half + 1):
                by = offs_ref[2 * length + d]
                mixed = jnp.where(lane >= by, here, ahead)
                value = low + pltpu.roll(mixed, lax.rem(LANES - by, LANES), 1)
                if 2 * length < total:
                    levels[at][block, d, pl.ds(0, wide)] = value
                else:
                    peak = value if peak is None else jnp.maximum(peak, value)
        return peak

    peak, done = None, set()
    for j in list(range(count // 2)) + list(reversed(range(count // 2, count))):
        slot = flip(me, j)
        arrived(slot)
        done.add(j)
        length = 1
        while length < rows:
            for inner in range(rows // (2 * length)):
                peak = node(length, slot * (rows // (2 * length)) + inner, slot, inner)
            length *= 2
        step = 1
        while step < count and done.issuperset(range(j // (2 * step) * 2 * step, (j // (2 * step) + 1) * 2 * step)):
            peak = node(step * rows, flip(lax.div(me, 2 * step), j // (2 * step)))
            step *= 2

    mine = pl.ds(me * tiles, tiles)
    out_ref[mine] = peak
    for j in range(1, count):
        both(j, lambda copy: copy.wait_send())
    if chans > 1:
        @pl.when(col > 0)
        def _():
            edge().wait_send()

    def result(j, t):
        part = out_ref.at[pl.ds(t * tiles, tiles)]
        return pltpu.make_async_remote_copy(
            src_ref=part,
            dst_ref=part,
            send_sem=send_sem2.at[j],
            recv_sem=recv_sem2.at[t],
            device_id=(flip(me, j), col),
            device_id_type=MESH,
        )

    for j in reversed(range(1, count)):
        result(j, me).start()
    for j in range(1, count):
        result(j, flip(me, j)).wait_recv()
    for j in range(1, count):
        result(j, me).wait_send()


def local(count, chans, spectrum, offsets):
    rows, span = spectrum.shape
    total = count * rows
    tiles = span // LANES // count
    halo = (total - 1 + LANES - 1) // LANES
    x = spectrum.reshape(rows, span // LANES, LANES).transpose(1, 0, 2)
    deep = round_up(tiles + halo, 8) + 8
    scratch = [pltpu.VMEM((count, deep, rows, LANES), jnp.float32)]
    length = 2
    while length < total:
        scratch.append(pltpu.VMEM((total // length, length, deep, LANES), jnp.float32))
        length *= 2
    dma = pltpu.SemaphoreType.DMA
    scratch += [dma((count,)), dma((count,)), dma((1,)), dma((count,)), dma((count,))]
    peak = pl.pallas_call(
        functools.partial(kernel, count, chans, rows, tiles, halo),
        out_shape=jax.ShapeDtypeStruct((count * tiles, LANES), jnp.float32),
        in_specs=[pl.BlockSpec(memory_space=pltpu.SMEM), pl.BlockSpec(memory_space=pl.ANY)],
        out_specs=pl.BlockSpec(memory_space=pltpu.VMEM),
        scratch_shapes=scratch,
        compiler_params=pltpu.CompilerParams(collective_id=0, has_side_effects=True),
    )(offsets, x)
    return peak.reshape(span)


def solution(mesh):
    body = functools.partial(local, mesh.shape["tm"], mesh.shape["chan"])
    placed = (P("tm", "chan"), P())
    return jax.shard_map(body, mesh=mesh, in_specs=placed, out_specs=P("chan"), check_vma=False)
```

profile of v0, /device:TPU:0, one launch (start us, length us, event | category | flops | bytes accessed | tf_op | source)
XLA Modules:
  0.0 30.2 jit_solution(5736958322554318421)
XLA Ops:
  0.0 28.5 %shard_map.28 = f32[512,128]{1,0:T(8,128)} custom-call(s32[64]{0:T(128)} %offs_ref.1, f32[512,2,128]{2,1,0:T(2,128)} %bitcast.5), custom_call_target="tpu_custom_call" | custom-call | tf_op jit(solution)/shard_map/pallas_call | solution.py:199
  28.5 1.7 %copy.4 = f32[65536]{0:T(1024)} copy(f32[65536]{0:T(1024)} %bitcast.4) | data formatting | bytes 524288
where the time goes:
time: 30.4 us; the launch traced here: 30.2 us
  Pallas kernels  28.5 us (94%)
  local copies, waits for them, and re-layouts  1.67 us (5%)
    pallas_call x1, Pallas kernels, local(): pl.pallas_call(functools.partial(kernel, count, chans, rows, tiles, halo)...  28.5 us
    unnamed x1, local copies, waits for them, and re-layouts  1.67 us

commit v1 on v0

v1 whole, which is shorter than its diff:
```python
import functools

import jax
import jax.numpy as jnp
from jax import lax
from jax.experimental import pallas as pl
from jax.experimental.pallas import tpu as pltpu
from jax.sharding import PartitionSpec as P

LANES = 128
MESH = pl.DeviceIdType.MESH


def round_up(value, to):
    return (value + to - 1) // to * to


def flip(place, bits):
    out, bit = place, 1
    while bit <= bits:
        if bits & bit:
            out = out + bit * (1 - 2 * lax.rem(lax.div(place, bit), 2))
        bit *= 2
    return out


def pieces(tiles):
    if tiles % 8 or tiles < 16:
        return [(0, tiles)]
    return [(0, tiles)]


def kernel(count, chans, rows, tiles, halo, cuts, offs_hbm, x_hbm, out_ref, offs_ref, x_ref, recv, *rest):
    levels = rest[:-8]
    offs_sem, x_sem, send_sem, recv_sem, edge_sem, peak_send, peak_recv, relay_send = rest[-8:]
    me = lax.axis_index("tm")
    col = lax.axis_index("chan")
    total = count * rows
    half = count // 2
    last = len(cuts) - 1
    at_end = me == count - 1
    no_next = me * chans + col == count * chans - 1

    offs_copy = pltpu.make_async_copy(offs_hbm, offs_ref, offs_sem)
    offs_copy.start()
    x_copy = pltpu.make_async_copy(x_hbm, x_ref, x_sem)
    x_copy.start()

    barrier = pltpu.get_barrier_semaphore()
    for j in reversed(range(1, count)):
        pl.semaphore_signal(barrier, inc=1, device_id=(flip(me, j), col), device_id_type=MESH)
    if chans > 1:
        @pl.when(jnp.logical_and(at_end, col < chans - 1))
        def _():
            for t in range(count):
                pl.semaphore_signal(barrier, inc=1, device_id=(t, jnp.minimum(col + 1, chans - 1)), device_id_type=MESH)

    def extent(c):
        at, width = cuts[c]
        return at, width, width + (halo if c == 0 else 0)

    def own(c, size):
        at = cuts[c][0]
        return pltpu.make_async_copy(
            x_hbm.at[pl.ds(me * tiles + at, size)], recv.at[me, pl.ds(at, size)], recv_sem.at[c, me]
        )

    for c in range(len(cuts)):
        at, width, full = extent(c)
        if full == width:
            own(c, width).start()
        else:
            @pl.when(at_end)
            def _():
                own(c, width).start()

            @pl.when(jnp.logical_not(at_end))
            def _():
                own(c, full).start()

    x_copy.wait()
    pl.semaphore_wait(barrier, count - 1 + jnp.where(col > 0, 1, 0))

    def to_peer(c, j, size):
        k, at = flip(me, j), cuts[c][0]
        return pltpu.make_async_remote_copy(
            src_ref=x_ref.at[pl.ds(k * tiles + at, size)],
            dst_ref=recv.at[me, pl.ds(at, size)],
            send_sem=send_sem.at[c, j],
            recv_sem=recv_sem.at[c, me],
            device_id=(k, col),
            device_id_type=MESH,
        )

    def to(c, j, act):
        at, width, full = extent(c)
        if full == width:
            act(to_peer(c, j, width))
            return

        @pl.when(flip(me, j) == count - 1)
        def _():
            act(to_peer(c, j, width))

        @pl.when(flip(me, j) != count - 1)
        def _():
            act(to_peer(c, j, full))

    def edge():
        return pltpu.make_async_remote_copy(
            src_ref=x_ref.at[pl.ds(0, halo)],
            dst_ref=recv.at[me, pl.ds(tiles, halo)],
            send_sem=edge_sem.at[0],
            recv_sem=recv_sem.at[0, me],
            device_id=(count - 1, jnp.maximum(col - 1, 0)),
            device_id_type=MESH,
        )

    if chans > 1:
        @pl.when(col > 0)
        def _():
            edge().start()

    for c in range(len(cuts)):
        for j in reversed(range(1, count)):
            to(c, j, lambda copy: copy.start())

    @pl.when(no_next)
    def _():
        for t in range(count):
            recv[t, pl.ds(tiles, halo)] = jnp.zeros((halo, rows, LANES), jnp.float32)

    offs_copy.wait()

    def arrived(c, t):
        at, width, full = extent(c)

        def wait(size):
            part = recv.at[t, pl.ds(at, size)]
            pltpu.make_async_copy(part, part, recv_sem.at[c, t]).wait()

        if full == width:
            wait(width)
            return

        @pl.when(no_next)
        def _():
            wait(width)

        @pl.when(jnp.logical_not(no_next))
        def _():
            wait(full)

    def node(c, length, block, slot=0, inner=0):
        base, width, _ = extent(c)
        at = length.bit_length() - 1
        wide = width + ((total - 2 * length + LANES - 1) // LANES if c == 0 else 0)
        lane = lax.broadcasted_iota(jnp.int32, (wide, LANES), 1)

        def load(which, d, start):
            if length == 1:
                return recv[slot, pl.ds(start, wide), 2 * inner + which]
            return levels[at - 1][2 * block + which, d, pl.ds(start, wide)]

        peak = None
        for pair in range(length):
            low = load(0, pair, base)
            here = load(1, pair, base)
            ahead = load(1, pair, base + 1)

            def moved(d):
                by = offs_ref[2 * length + d]
                return pltpu.roll(jnp.where(lane >= by, here, ahead), lax.rem(LANES - by, LANES), 1)

            if 2 * length < total:
                for d in (2 * pair, 2 * pair + 1):
                    levels[at][block, d, pl.ds(base, wide)] = low + moved(d)
            else:
                value = low + jnp.maximum(moved(2 * pair), moved(2 * pair + 1))
                peak = value if peak is None else jnp.maximum(peak, value)
        return peak

    def result(c, owner, send, j):
        at, width = cuts[c]
        part = out_ref.at[pl.ds(owner * tiles + at, width)]
        return pltpu.make_async_remote_copy(
            src_ref=part,
            dst_ref=part,
            send_sem=send,
            recv_sem=peak_recv.at[c, owner],
            device_id=(flip(me, j), col),
            device_id_type=MESH,
        )

    def mine(c):
        return list(reversed(range(1, count)))

    for c in range(len(cuts)):
        peak, done = None, set()
        for j in list(range(half)) + list(reversed(range(half, count))):
            slot = flip(me, j)
            arrived(c, slot)
            done.add(j)
            length = 1
            while length < rows:
                for inner in range(rows // (2 * length)):
                    peak = node(c, length, slot * (rows // (2 * length)) + inner, slot, inner)
                length *= 2
            step = 1
            while step < count and done.issuperset(range(j // (2 * step) * 2 * step, (j // (2 * step) + 1) * 2 * step)):
                peak = node(c, step * rows, flip(lax.div(me, 2 * step), j // (2 * step)))
                step *= 2
        at, width = cuts[c]
        out_ref[pl.ds(me * tiles + at, width)] = peak
        for j in mine(c):
            result(c, me, peak_send.at[c, j], j).start()

    for c in range(0):
        owner = flip(me, half)
        result(c, owner, peak_send.at[c, half], half).wait_recv()
        for j in range(1, half):
            result(c, owner, relay_send.at[c, j], j).start()

    for c in range(len(cuts)):
        for j in range(1, count):
            to(c, j, lambda copy: copy.wait_send())
    if chans > 1:
        @pl.when(col > 0)
        def _():
            edge().wait_send()
    for c in range(len(cuts)):
        for j in mine(c):
            result(c, me, peak_send.at[c, j], j).wait_send()
        if False:
            for j in range(1, half):
                result(c, me, relay_send.at[c, j], j).wait_send()
    for c in range(len(cuts)):
        for j in range(1, count):
            if True:
                result(c, flip(me, j), peak_send.at[c, j], j).wait_recv()


def local(count, chans, spectrum, offsets):
    rows, span = spectrum.shape
    total = count * rows
    tiles = span // LANES // count
    halo = (total - 1 + LANES - 1) // LANES
    cuts = pieces(tiles)
    x = spectrum.reshape(rows, span // LANES, LANES).transpose(1, 0, 2)
    deep = round_up(tiles + halo, 8) + 8
    scratch = [
        pltpu.SMEM(offsets.shape, jnp.int32),
        pltpu.VMEM(x.shape, jnp.float32),
        pltpu.VMEM((count, deep, rows, LANES), jnp.float32),
    ]
    length = 2
    while length < total:
        scratch.append(pltpu.VMEM((total // length, length, deep, LANES), jnp.float32))
        length *= 2
    dma = pltpu.SemaphoreType.DMA
    every = dma((len(cuts), count))
    scratch += [dma, dma, every, every, dma((1,)), every, every, every]
    peak = pl.pallas_call(
        functools.partial(kernel, count, chans, rows, tiles, halo, cuts),
        out_shape=jax.ShapeDtypeStruct((count * tiles, LANES), jnp.float32),
        in_specs=[pl.BlockSpec(memory_space=pltpu.HBM), pl.BlockSpec(memory_space=pltpu.HBM)],
        out_specs=pl.BlockSpec(memory_space=pltpu.VMEM),
        scratch_shapes=scratch,
        compiler_params=pltpu.CompilerParams(collective_id=0, has_side_effects=True, vmem_limit_bytes=40 * 2**20),
    )(pltpu.with_memory_space_constraint(offsets, pltpu.HBM), pltpu.with_memory_space_constraint(x, pltpu.HBM))
    return peak.reshape(span)


def solution(mesh):
    body = functools.partial(local, mesh.shape["tm"], mesh.shape["chan"])
    placed = (P("tm", "chan"), P())
    return jax.shard_map(body, mesh=mesh, in_specs=placed, out_specs=P("chan"), check_vma=False)
```

time: 30.4 us -> 27.8 us (0.914)
  Pallas kernels: 28.5 us -> 27 us
  local copies, waits for them, and re-layouts: 1.67 us -> 0.72 us
    pallas_call x1, Pallas kernels: 28.5 us -> 27 us  [local(): pl.pallas_call(functools.partial(kernel, count, chans, rows, tiles, halo,...]
    unnamed x1, local copies, waits for them, and re-layouts: 1.67 us -> 0.72 us
where the time goes in v1:
time: 27.8 us; the launch traced here: 27.7 us
  Pallas kernels  27 us (97%)
  local copies, waits for them, and re-layouts  0.72 us (3%)
    pallas_call x1, Pallas kernels, local(): pl.pallas_call(functools.partial(kernel, count, chans, rows, tiles, halo,...  27 us
    unnamed x1, local copies, waits for them, and re-layouts  0.72 us

profile of v1, /device:TPU:0, one launch (start us, length us, event | category | flops | bytes accessed | tf_op | source)
XLA Modules:
  0.0 27.7 jit_solution(1414785340701033142)
XLA Ops:
  0.0 27.0 %shard_map.28 = f32[512,128]{1,0:T(8,128)S(1)} custom-call(s32[64]{0:T(128)} %offs_hbm.1, f32[512,2,128]{2,1,0:T(2,128)} %bitcast.5), custom_call_target="tpu_custom_call" | custom-call | tf_op jit(solution)/shard_map/pallas_call | solution.py:263
  27.0 0.7 %copy.4 = f32[65536]{0:T(1024)} copy(f32[65536]{0:T(1024)S(1)} %bitcast.4) | data formatting | bytes 524288

commit v2 on v0

v2 whole, which is shorter than its diff:
```python
import functools

import jax
import jax.numpy as jnp
from jax import lax
from jax.experimental import pallas as pl
from jax.experimental.pallas import tpu as pltpu
from jax.sharding import PartitionSpec as P

LANES = 128
LAYERS = 4
MESH = pl.DeviceIdType.MESH


def round_up(value, to):
    return (value + to - 1) // to * to


def flip(place, bits):
    out, bit = place, 1
    while bit <= bits:
        if bits & bit:
            out = out + bit * (1 - 2 * lax.rem(lax.div(place, bit), 2))
        bit *= 2
    return out


def kernel(count, chans, rows, tiles, halo, offs_hbm, x_hbm, out_ref, offs_ref, x_ref, recv, *rest):
    levels = rest[:-9]
    offs_sem, x_sem, send_sem, recv_sem, edge_send, edge_recv, peak_send, peak_recv, known = rest[-9:]
    me = lax.axis_index("tm")
    col = lax.axis_index("chan")
    total = count * rows
    quarter = count // LAYERS
    half = 2 * quarter
    span = count * tiles
    full = tiles + halo

    offs_copy = pltpu.make_async_copy(offs_hbm, offs_ref, offs_sem)
    offs_copy.start()
    x_copy = pltpu.make_async_copy(x_hbm, x_ref.at[pl.ds(0, span)], x_sem)
    x_copy.start()

    barrier = pltpu.get_barrier_semaphore()
    for d in (3, 2, 1):
        pl.semaphore_signal(barrier, inc=1, device_id=(flip(me, d * quarter), col), device_id_type=MESH)
    for q in reversed(range(1, quarter)):
        pl.semaphore_signal(barrier, inc=1, device_id=(flip(me, q), col), device_id_type=MESH)
    if chans > 1:
        @pl.when(col < chans - 1)
        def _():
            pl.semaphore_signal(barrier, inc=1, device_id=(me, jnp.minimum(col + 1, chans - 1)), device_id_type=MESH)

    @pl.when(col == chans - 1)
    def _():
        x_ref[pl.ds(span, halo)] = jnp.zeros((halo, rows, LANES), jnp.float32)

    def own(act):
        def sized(size):
            act(
                pltpu.make_async_copy(
                    x_hbm.at[pl.ds(me * tiles, size)], recv.at[me, pl.ds(0, size)], recv_sem.at[me]
                )
            )

        @pl.when(me == count - 1)
        def _():
            sized(tiles)

        @pl.when(me != count - 1)
        def _():
            sized(full)

    def target(j):
        return flip(me, j)

    def to(j):
        k = target(j)
        return pltpu.make_async_remote_copy(
            src_ref=x_ref.at[pl.ds(k * tiles, full)],
            dst_ref=recv.at[me, pl.ds(0, full)],
            send_sem=send_sem.at[j],
            recv_sem=recv_sem.at[me],
            device_id=(k, col),
            device_id_type=MESH,
        )

    def edge():
        return pltpu.make_async_remote_copy(
            src_ref=x_ref.at[pl.ds(0, halo)],
            dst_ref=x_ref.at[pl.ds(span, halo)],
            send_sem=edge_send,
            recv_sem=edge_recv,
            device_id=(me, jnp.maximum(col - 1, 0)),
            device_id_type=MESH,
        )

    x_copy.wait()
    pl.semaphore_wait(barrier, LAYERS - 1 + quarter - 1 + jnp.where(col > 0, 1, 0))
    for q in reversed(range(1, quarter)):
        pl.semaphore_signal(known, inc=1, device_id=(flip(me, q), col), device_id_type=MESH)
    if chans > 1:
        @pl.when(col > 0)
        def _():
            edge().start()

    early = [3 * quarter, 2 * quarter]
    for j in early:
        @pl.when(target(j) != count - 1)
        def _():
            to(j).start()

    pl.semaphore_wait(known, quarter - 1)
    if chans > 1:
        @pl.when(col < chans - 1)
        def _():
            edge().wait_recv()
    for j in early:
        @pl.when(target(j) == count - 1)
        def _():
            to(j).start()
    for j in list(reversed(range(1, count))):
        if j not in early:
            to(j).start()

    own(lambda copy: copy.start())
    offs_copy.wait()

    @pl.when(me == count - 1)
    def _():
        recv[me, pl.ds(tiles, halo)] = x_ref[pl.ds(span, halo)]

    def arrived(t):
        part = recv.at[t, pl.ds(0, full)]
        pltpu.make_async_copy(part, part, recv_sem.at[t]).wait()

    def node(length, block, slot=0, part=0):
        at = length.bit_length() - 1
        wide = tiles + (total - 2 * length + LANES - 1) // LANES
        lane = lax.broadcasted_iota(jnp.int32, (wide, LANES), 1)

        def load(which, d, start):
            if length == 1:
                return recv[slot, pl.ds(start, wide), 2 * part + which]
            return levels[at - 1][2 * block + which, d, pl.ds(start, wide)]

        peak = None
        for pair in range(length):
            low = load(0, pair, 0)
            here = load(1, pair, 0)
            ahead = load(1, pair, 1)

            def moved(d):
                by = offs_ref[2 * length + d]
                return pltpu.roll(jnp.where(lane >= by, here, ahead), lax.rem(LANES - by, LANES), 1)

            if 2 * length < total:
                for d in (2 * pair, 2 * pair + 1):
                    levels[at][block, d, pl.ds(0, wide)] = low + moved(d)
            else:
                value = low + jnp.maximum(moved(2 * pair), moved(2 * pair + 1))
                peak = value if peak is None else jnp.maximum(peak, value)
        return peak

    peak, done = None, set()
    for group in [range(0, quarter), range(quarter, half), range(half, count)]:
        for j in group:
            if j:
                arrived(flip(me, j))
            else:
                own(lambda copy: copy.wait())
        done.update(group)
        length = 1
        while length < rows:
            for j in group:
                slot = flip(me, j)
                for part in range(rows // (2 * length)):
                    peak = node(length, slot * (rows // (2 * length)) + part, slot, part)
            length *= 2
        step = 1
        while step < count:
            for first in sorted({j // (2 * step) for j in group}):
                if done.issuperset(range(first * 2 * step, (first + 1) * 2 * step)):
                    peak = node(step * rows, flip(lax.div(me, 2 * step), first))
            step *= 2

    out_ref[pl.ds(me * tiles, tiles)] = peak

    def share(j, owner):
        part = out_ref.at[pl.ds(owner * tiles, tiles)]
        return pltpu.make_async_remote_copy(
            src_ref=part,
            dst_ref=part,
            send_sem=peak_send.at[j],
            recv_sem=peak_recv.at[owner],
            device_id=(flip(me, j), col),
            device_id_type=MESH,
        )

    for j in list(reversed(range(1, count))):
        share(j, me).start()
    for j in range(1, count):
        to(j).wait_send()
    if chans > 1:
        @pl.when(col > 0)
        def _():
            edge().wait_send()
    for j in list(reversed(range(1, count))):
        share(j, flip(me, j)).wait_recv()
    for j in list(reversed(range(1, count))):
        share(j, me).wait_send()


def local(count, chans, spectrum, offsets):
    rows, span = spectrum.shape
    total = count * rows
    tiles = span // LANES // count
    halo = (total - 1 + LANES - 1) // LANES
    x = spectrum.reshape(rows, span // LANES, LANES).transpose(1, 0, 2)
    deep = round_up(tiles + halo, 8) + 8
    scratch = [
        pltpu.SMEM(offsets.shape, jnp.int32),
        pltpu.VMEM((x.shape[0] + halo, rows, LANES), jnp.float32),
        pltpu.VMEM((count, deep, rows, LANES), jnp.float32),
    ]
    length = 2
    while length < total:
        scratch.append(pltpu.VMEM((total // length, length, deep, LANES), jnp.float32))
        length *= 2
    dma = pltpu.SemaphoreType.DMA
    each = dma((count,))
    scratch += [dma, dma, each, each, dma, dma, each, each, pltpu.SemaphoreType.REGULAR]
    keep = functools.partial(pltpu.with_memory_space_constraint, memory_space=pltpu.HBM)
    peak = pl.pallas_call(
        functools.partial(kernel, count, chans, rows, tiles, halo),
        out_shape=jax.ShapeDtypeStruct((count * tiles, LANES), jnp.float32),
        in_specs=[pl.BlockSpec(memory_space=pltpu.HBM), pl.BlockSpec(memory_space=pltpu.HBM)],
        out_specs=pl.BlockSpec(memory_space=pltpu.VMEM),
        scratch_shapes=scratch,
        compiler_params=pltpu.CompilerParams(collective_id=0, has_side_effects=True, vmem_limit_bytes=40 * 2**20),
    )(keep(offsets), keep(x))
    return peak.reshape(span)


def solution(mesh):
    body = functools.partial(local, mesh.shape["tm"], mesh.shape["chan"])
    placed = (P("tm", "chan"), P())
    return jax.shard_map(body, mesh=mesh, in_specs=placed, out_specs=P("chan"), check_vma=False)
```

time: 30.4 us -> 26.7 us (0.88)
  Pallas kernels: 28.5 us -> 25.8 us
  local copies, waits for them, and re-layouts: 1.67 us -> 0.72 us
    pallas_call x1, Pallas kernels: 28.5 us -> 25.8 us  [local(): pl.pallas_call(functools.partial(kernel, count, chans, rows, tiles, halo)...]
    unnamed x1, local copies, waits for them, and re-layouts: 1.67 us -> 0.72 us
where the time goes in v2:
time: 26.7 us; the launch traced here: 26.5 us
  Pallas kernels  25.8 us (97%)
  local copies, waits for them, and re-layouts  0.72 us (3%)
    pallas_call x1, Pallas kernels, local(): pl.pallas_call(functools.partial(kernel, count, chans, rows, tiles, halo)...  25.8 us
    unnamed x1, local copies, waits for them, and re-layouts  0.72 us

profile of v2, /device:TPU:0, one launch (start us, length us, event | category | flops | bytes accessed | tf_op | source)
XLA Modules:
  0.0 26.5 jit_solution(10066714727787692069)
XLA Ops:
  0.0 25.8 %shard_map.28 = f32[512,128]{1,0:T(8,128)S(1)} custom-call(s32[64]{0:T(128)} %offs_hbm.1, f32[512,2,128]{2,1,0:T(2,128)} %bitcast.5), custom_call_target="tpu_custom_call" | custom-call | tf_op jit(solution)/shard_map/pallas_call | solution.py:234
  25.8 0.7 %copy.4 = f32[65536]{0:T(1024)} copy(f32[65536]{0:T(1024)S(1)} %bitcast.4) | data formatting | bytes 524288

commit v3 on v2

--- a/solution.py
+++ b/solution.py
@@ -163,7 +163,7 @@
         return peak
 
     peak, done = None, set()
-    for group in [range(0, quarter), range(quarter, half), range(half, count)]:
+    for group in [range(first, first + quarter) for first in (0, quarter, 3 * quarter, 2 * quarter)]:
         for j in group:
             if j:
                 arrived(flip(me, j))
@@ -197,8 +197,25 @@
             device_id_type=MESH,
         )
 
-    for j in list(reversed(range(1, count))):
-        share(j, me).start()
+    def share_first():
+        part = out_ref.at[pl.ds(me * tiles, tiles)]
+        return pltpu.make_async_remote_copy(
+            src_ref=part,
+            dst_ref=part,
+            send_sem=peak_send.at[me],
+            recv_sem=peak_recv.at[me],
+            device_id=(0, col),
+            device_id_type=MESH,
+        )
+
+    @pl.when(me != 0)
+    def _():
+        share_first().start()
+
+    for j in list(reversed(range(quarter, half))) + list(reversed(range(half, count))) + list(reversed(range(1, quarter))):
+        @pl.when(me != j)
+        def _():
+            share(j, me).start()
     for j in range(1, count):
         to(j).wait_send()
     if chans > 1:

time: 26.7 us -> 26.2 us (0.981)
  Pallas kernels: 25.8 us -> 25.3 us
    pallas_call x1, Pallas kernels: 25.8 us -> 25.3 us  [local(): pl.pallas_call(functools.partial(kernel, count, chans, rows, tiles, halo)...]
where the time goes in v3:
time: 26.2 us; the launch traced here: 26.1 us
  Pallas kernels  25.3 us (97%)
  local copies, waits for them, and re-layouts  0.72 us (3%)
    pallas_call x1, Pallas kernels, local(): pl.pallas_call(functools.partial(kernel, count, chans, rows, tiles, halo)...  25.3 us
    unnamed x1, local copies, waits for them, and re-layouts  0.72 us

profile of v3, /device:TPU:0, one launch (start us, length us, event | category | flops | bytes accessed | tf_op | source)
XLA Modules:
  0.0 26.1 jit_solution(3615551575339725926)
XLA Ops:
  0.0 25.3 %shard_map.28 = f32[512,128]{1,0:T(8,128)S(1)} custom-call(s32[64]{0:T(128)} %offs_hbm.1, f32[512,2,128]{2,1,0:T(2,128)} %bitcast.5), custom_call_target="tpu_custom_call" | custom-call | tf_op jit(solution)/shard_map/pallas_call | solution.py:251
  25.3 0.7 %copy.4 = f32[65536]{0:T(1024)} copy(f32[65536]{0:T(1024)S(1)} %bitcast.4) | data formatting | bytes 524288

commit v4 on v3

--- a/solution.py
+++ b/solution.py
@@ -163,7 +163,7 @@
         return peak
 
     peak, done = None, set()
-    for group in [range(first, first + quarter) for first in (0, quarter, 3 * quarter, 2 * quarter)]:
+    for group in [range(0, half), range(half + quarter, count), range(half, half + quarter)]:
         for j in group:
             if j:
                 arrived(flip(me, j))

time: 26.2 us -> 26.2 us (level)
  no operation moved by 1% of the time
where the time goes in v4:
time: 26.2 us; the launch traced here: 26.1 us
  Pallas kernels  25.3 us (97%)
  local copies, waits for them, and re-layouts  0.72 us (3%)
    pallas_call x1, Pallas kernels, local(): pl.pallas_call(functools.partial(kernel, count, chans, rows, tiles, halo)...  25.3 us
    unnamed x1, local copies, waits for them, and re-layouts  0.72 us

profile of v4, /device:TPU:0, one launch (start us, length us, event | category | flops | bytes accessed | tf_op | source)
XLA Modules:
  0.0 26.1 jit_solution(16820542356279649043)
XLA Ops:
  0.0 25.3 %shard_map.28 = f32[512,128]{1,0:T(8,128)S(1)} custom-call(s32[64]{0:T(128)} %offs_hbm.1, f32[512,2,128]{2,1,0:T(2,128)} %bitcast.5), custom_call_target="tpu_custom_call" | custom-call | tf_op jit(solution)/shard_map/pallas_call | solution.py:251
  25.3 0.7 %copy.4 = f32[65536]{0:T(1024)} copy(f32[65536]{0:T(1024)S(1)} %bitcast.4) | data formatting | bytes 524288
